TPU v7x, 32 devices: a whole 2x2x4 slice. The times are simulated.
32 devices in a mesh: gene: 8 (over z, x), cell: 4 (over y, core).
Axes of the slice: x: 2, y: 2, z: 4, core: 2. Of those that a mesh axis runs over, the one named last changes fastest.
Arguments:
- pool_counts: bfloat16 [20480, 16384], P('gene', 'cell'), may hold values from 0 to 6.5
- cell_picks: int32 [7, 4096], P(None, 'cell'), may hold values from 0 to 16383, as said below
- loadings_init: float32 [64, 20480], P(None, 'gene'), may hold values from -0.0390625 to 0.0390625
Outputs:
- scaled_loadings: float32 [64, 20480], P(None, 'gene')
Inputs may be any that keep to these rules, and one draw needn't show every extreme that they name: `cell_picks`: column b of every row names a pool cell in [(b // 1024) * 4096, (b // 1024 + 1) * 4096); no cell is named twice in one row.
All inputs are finite; a program needn't handle non-finite values.
Results may differ from a plain program's by a relative error of at most 0.018.
Values may be sent and summed in bfloat16 or wider, within the bound.
A program may use at most 128 MiB of HBM per device.

v0:
```python
import math

import jax
import jax.numpy as jnp
from jax import lax
from jax.sharding import PartitionSpec as P

STEPS = 7


step_rate = 1.0


def transposed_product(left, right):
    return lax.dot_general(
        left, right, (((1,), (1,)), ((), ())), preferred_element_type=jnp.float32
    )


def shards(pool_counts, cell_picks, loadings_init):
    loadings = loadings_init
    local_pool = pool_counts.shape[1]
    group = lax.axis_index("cell")
    batch_total = cell_picks.shape[1] * lax.axis_size("cell")
    gene_total = loadings.shape[1] * lax.axis_size("gene")
    for step_index in range(STEPS):
        chosen = cell_picks[step_index] - group * local_pool
        gathered = jnp.take(pool_counts, chosen, axis=1)
        weights_low = loadings.astype(jnp.bfloat16)
        product = jnp.dot(weights_low, gathered, preferred_element_type=jnp.float32)
        local_sums = jnp.sum(gathered, axis=1, dtype=jnp.float32)
        batch_means = lax.psum(local_sums, "cell") / batch_total
        shift = jnp.dot(
            weights_low.astype(jnp.float32), batch_means, precision=lax.Precision.HIGHEST
        )
        partial_value = product - shift[:, None]
        scores = lax.psum(partial_value, "gene")
        scores_low = scores.astype(jnp.bfloat16)
        raw_update = transposed_product(scores_low, gathered)
        row_totals = jnp.sum(scores_low, axis=1, dtype=jnp.float32)
        local_update = (raw_update - row_totals[:, None] * batch_means[None, :]) / batch_total
        update = lax.psum(local_update.astype(jnp.bfloat16), "cell").astype(jnp.float32)
        stepped = loadings + step_rate * update
        gram_part = jnp.dot(stepped, stepped.T, precision=lax.Precision.HIGHEST)
        gram_matrix = lax.psum(gram_part, "gene")
        factor = jnp.linalg.cholesky(gram_matrix)
        loadings = lax.linalg.triangular_solve(factor, stepped, left_side=True, lower=True)
    return loadings * math.sqrt(gene_total)


def solution(mesh):
    placed = (P("gene", "cell"), P(None, "cell"), P(None, "gene"))
    return jax.shard_map(
        shards, mesh=mesh, in_specs=placed, out_specs=P(None, "gene"), check_vma=False
    )
```

profile of v0, /device:TPU:0, one launch (start us, length us, event | category | flops | bytes accessed | tf_op | source)
XLA Modules:
  0.0 1143.6 jit_solution(7488319310404820462)
XLA Ops:
  7.8 25.9 %copy.4 = bf16[2560,4096]{0,1:T(8,128)(2,1)} copy(bf16[2560,4096]{1,0:T(8,128)(2,1)} %param.8) | data formatting | bytes 41943040 | tf_op args[0]
  33.7 20.2 %gather_fusion.6 = bf16[1024,2560]{1,0:T(8,128)(2,1)} fusion(bf16[2560,4096]{0,1:T(8,128)(2,1)} %copy.4, s32[1024]{0:T(1024)S(1)} %fusion.188), kind=kCustom, calls=%fused_computation.6.clone | custom fusion | bytes 10489856 | tf_op jit(solution)/shard_map/jit(_take)/gather | solution.py:28
  53.8 20.1 %gather_fusion.5 = bf16[1024,2560]{1,0:T(8,128)(2,1)} fusion(bf16[2560,4096]{0,1:T(8,128)(2,1)} %copy.4, s32[1024]{0:T(1024)S(1)} %fusion.187), kind=kCustom, calls=%fused_computation.5.clone | custom fusion | bytes 10489856 | tf_op jit(solution)/shard_map/jit(_take)/gather | solution.py:28
  73.9 20.3 %gather_fusion.4 = bf16[1024,2560]{1,0:T(8,128)(2,1)} fusion(bf16[2560,4096]{0,1:T(8,128)(2,1)} %copy.4, s32[1024]{0:T(1024)S(1)} %fusion.186), kind=kCustom, calls=%fused_computation.4.clone | custom fusion | bytes 10489856 | tf_op jit(solution)/shard_map/jit(_take)/gather | solution.py:28
  94.2 20.1 %gather_fusion.3 = bf16[1024,2560]{1,0:T(8,128)(2,1)} fusion(bf16[2560,4096]{0,1:T(8,128)(2,1)} %copy.4, s32[1024]{0:T(1024)S(1)} %fusion.185), kind=kCustom, calls=%fused_computation.3.clone | custom fusion | bytes 10489856 | tf_op jit(solution)/shard_map/jit(_take)/gather | solution.py:28
  114.3 20.3 %gather_fusion.2 = bf16[1024,2560]{1,0:T(8,128)(2,1)} fusion(bf16[2560,4096]{0,1:T(8,128)(2,1)} %copy.4, s32[1024]{0:T(1024)S(1)} %fusion.184), kind=kCustom, calls=%fused_computation.2.clone | custom fusion | bytes 10489856 | tf_op jit(solution)/shard_map/jit(_take)/gather | solution.py:28
  134.6 20.1 %gather_fusion.1 = bf16[1024,2560]{1,0:T(8,128)(2,1)} fusion(bf16[2560,4096]{0,1:T(8,128)(2,1)} %copy.4, s32[1024]{0:T(1024)S(1)} %fusion.183), kind=kCustom, calls=%fused_computation.1.clone | custom fusion | bytes 10489856 | tf_op jit(solution)/shard_map/jit(_take)/gather | solution.py:28
  154.7 20.1 %gather_fusion = bf16[1024,2560]{1,0:T(8,128)(2,1)} fusion(bf16[2560,4096]{0,1:T(8,128)(2,1)} %copy.4, s32[1024]{0:T(1024)S(1)} %fusion.182), kind=kCustom, calls=%fused_computation.clone | custom fusion | bytes 10489856 | tf_op jit(solution)/shard_map/jit(_take)/gather | solution.py:28
  179.1 7.3 convert_reduce_fusion
  186.3 5.4 convert_reduce_fusion.2
  195.6 33.5 %all-reduce.31.cloned.1.call-done = (f32[2560]{0:T(1024)}, f32[2560]{0:T(1024)}, f32[2560]{0:T(1024)}, f32[2560]{0:T(1024)}, f32[2560]{0:T(1024)}, /*index=5*/f32[2560]{0:T(1024)}, f32[2560]{0:T(1024)}) async-done(((f32[2560]{0:T(1024)}, f32[2560]{0:T(1024)}, f32[2560]{0:T(1024)}, f32[2560]{0:T(1024)}, f32[2560]{0:T(1024)}, /*index=5*/f32[2560]{0:T(1024)}, f32[2560]{0:T(1024)}), (f32[2560]{0:T(1024)}, ...) | async-done | bytes 71696 | tf_op jit(solution)/shard_map/psum | solution.py:32
  234.5 40.7 %all-reduce.32 = bf16[64,1024]{1,0:T(8,128)(2,1)S(1)} all-reduce(f32[64,1024]{1,0:T(8,128)S(1)} %fusion.94), channel_id=1, replica_groups=mesh['gene'=8,'cell'=4] {'gene'}, use_global_device_ids=true, to_apply=%region_2.4 | all-reduce | flops 65536 | bytes 393216 | tf_op jit(solution)/shard_map/psum | solution.py:37
  279.8 30.3 %all-reduce.17.cloned.1.call-done = bf16[64,2560]{1,0:T(8,128)(2,1)} async-done(((bf16[64,2560]{1,0:T(8,128)(2,1)}), bf16[64,2560]{1,0:T(8,128)(2,1)}) %all-reduce.17.cloned.1.call-update) | async-done | bytes 327696 | tf_op jit(solution)/shard_map/psum | solution.py:42
  311.9 37.1 %psum.199 = f32[64,64]{0,1:T(8,128)S(1)} all-reduce(f32[64,64]{0,1:T(8,128)S(1)} %fusion.116), channel_id=1, replica_groups=mesh['gene'=8,'cell'=4] {'gene'}, use_global_device_ids=true, to_apply=%region_5.7 | all-reduce | flops 4096 | bytes 32768 | tf_op jit(solution)/shard_map/psum | solution.py:45
  349.1 5.8 cholesky.119
  356.3 4.9 custom-call.11
  367.6 36.0 %all-reduce.33 = bf16[64,1024]{1,0:T(8,128)(2,1)S(1)} all-reduce(f32[64,1024]{1,0:T(8,128)S(1)} %fusion.97), channel_id=1, replica_groups=mesh['gene'=8,'cell'=4] {'gene'}, use_global_device_ids=true, to_apply=%region_10.0 | all-reduce | flops 65536 | bytes 393216 | tf_op jit(solution)/shard_map/psum | solution.py:37
  408.3 30.5 %all-reduce.19.cloned.1.call-done = bf16[64,2560]{1,0:T(8,128)(2,1)} async-done(((bf16[64,2560]{1,0:T(8,128)(2,1)}), bf16[64,2560]{1,0:T(8,128)(2,1)}) %all-reduce.19.cloned.1.call-update) | async-done | bytes 327696 | tf_op jit(solution)/shard_map/psum | solution.py:42
  440.6 37.4 %psum.203 = f32[64,64]{0,1:T(8,128)S(1)} all-reduce(f32[64,64]{0,1:T(8,128)S(1)} %fusion.118), channel_id=1, replica_groups=mesh['gene'=8,'cell'=4] {'gene'}, use_global_device_ids=true, to_apply=%region_13.0 | all-reduce | flops 4096 | bytes 32768 | tf_op jit(solution)/shard_map/psum | solution.py:45
  478.0 5.8 cholesky.130
  485.2 4.9 custom-call.12
  496.5 36.0 %all-reduce.34 = bf16[64,1024]{1,0:T(8,128)(2,1)S(1)} all-reduce(f32[64,1024]{1,0:T(8,128)S(1)} %fusion.100), channel_id=1, replica_groups=mesh['gene'=8,'cell'=4] {'gene'}, use_global_device_ids=true, to_apply=%region_16.0 | all-reduce | flops 65536 | bytes 393216 | tf_op jit(solution)/shard_map/psum | solution.py:37
  532.7 4.4 fusion.76
  537.2 30.5 %all-reduce.21.cloned.1.call-done = bf16[64,2560]{1,0:T(8,128)(2,1)} async-done(((bf16[64,2560]{1,0:T(8,128)(2,1)}), bf16[64,2560]{1,0:T(8,128)(2,1)}) %all-reduce.21.cloned.1.call-update) | async-done | bytes 327696 | tf_op jit(solution)/shard_map/psum | solution.py:42
  569.5 37.1 %psum.207 = f32[64,64]{0,1:T(8,128)S(1)} all-reduce(f32[64,64]{0,1:T(8,128)S(1)} %fusion.120), channel_id=1, replica_groups=mesh['gene'=8,'cell'=4] {'gene'}, use_global_device_ids=true, to_apply=%region_19.0 | all-reduce | flops 4096 | bytes 32768 | tf_op jit(solution)/shard_map/psum | solution.py:45
  606.7 5.8 cholesky.141
  613.9 4.9 custom-call.13
  625.1 36.0 %all-reduce.35 = bf16[64,1024]{1,0:T(8,128)(2,1)S(1)} all-reduce(f32[64,1024]{1,0:T(8,128)S(1)} %fusion.103), channel_id=1, replica_groups=mesh['gene'=8,'cell'=4] {'gene'}, use_global_device_ids=true, to_apply=%region_22.0 | all-reduce | flops 65536 | bytes 393216 | tf_op jit(solution)/shard_map/psum | solution.py:37
  661.3 4.4 fusion.79
  666.0 30.4 %all-reduce.23.cloned.1.call-done = bf16[64,2560]{1,0:T(8,128)(2,1)} async-done(((bf16[64,2560]{1,0:T(8,128)(2,1)}), bf16[64,2560]{1,0:T(8,128)(2,1)}) %all-reduce.23.cloned.1.call-update) | async-done | bytes 327696 | tf_op jit(solution)/shard_map/psum | solution.py:42
  698.2 37.1 %psum.211 = f32[64,64]{0,1:T(8,128)S(1)} all-reduce(f32[64,64]{0,1:T(8,128)S(1)} %fusion.122), channel_id=1, replica_groups=mesh['gene'=8,'cell'=4] {'gene'}, use_global_device_ids=true, to_apply=%region_25.0 | all-reduce | flops 4096 | bytes 32768 | tf_op jit(solution)/shard_map/psum | solution.py:45
  735.4 5.8 cholesky.152
  742.6 4.9 custom-call.14
  753.9 36.0 %all-reduce.36 = bf16[64,1024]{1,0:T(8,128)(2,1)S(1)} all-reduce(f32[64,1024]{1,0:T(8,128)S(1)} %fusion.106), channel_id=1, replica_groups=mesh['gene'=8,'cell'=4] {'gene'}, use_global_device_ids=true, to_apply=%region_28.0 | all-reduce | flops 65536 | bytes 393216 | tf_op jit(solution)/shard_map/psum | solution.py:37
  794.5 30.6 %all-reduce.25.cloned.1.call-done = bf16[64,2560]{1,0:T(8,128)(2,1)} async-done(((bf16[64,2560]{1,0:T(8,128)(2,1)}), bf16[64,2560]{1,0:T(8,128)(2,1)}) %all-reduce.25.cloned.1.call-update) | async-done | bytes 327696 | tf_op jit(solution)/shard_map/psum | solution.py:42
  826.9 37.1 %psum.215 = f32[64,64]{0,1:T(8,128)S(1)} all-reduce(f32[64,64]{0,1:T(8,128)S(1)} %fusion.124), channel_id=1, replica_groups=mesh['gene'=8,'cell'=4] {'gene'}, use_global_device_ids=true, to_apply=%region_31.0 | all-reduce | flops 4096 | bytes 32768 | tf_op jit(solution)/shard_map/psum | solution.py:45
  864.1 5.8 cholesky.163
  871.3 4.9 custom-call.15
  882.6 36.3 %all-reduce.37 = bf16[64,1024]{1,0:T(8,128)(2,1)S(1)} all-reduce(f32[64,1024]{1,0:T(8,128)S(1)} %fusion.109), channel_id=1, replica_groups=mesh['gene'=8,'cell'=4] {'gene'}, use_global_device_ids=true, to_apply=%region_34.0 | all-reduce | flops 65536 | bytes 393216 | tf_op jit(solution)/shard_map/psum | solution.py:37
  923.5 30.6 %all-reduce.27.cloned.1.call-done = bf16[64,2560]{1,0:T(8,128)(2,1)} async-done(((bf16[64,2560]{1,0:T(8,128)(2,1)}), bf16[64,2560]{1,0:T(8,128)(2,1)}) %all-reduce.27.cloned.1.call-update) | async-done | bytes 327696 | tf_op jit(solution)/shard_map/psum | solution.py:42
  955.9 37.1 %psum.219 = f32[64,64]{0,1:T(8,128)S(1)} all-reduce(f32[64,64]{0,1:T(8,128)S(1)} %fusion.126), channel_id=1, replica_groups=mesh['gene'=8,'cell'=4] {'gene'}, use_global_device_ids=true, to_apply=%region_37.0 | all-reduce | flops 4096 | bytes 32768 | tf_op jit(solution)/shard_map/psum | solution.py:45
  993.1 5.8 cholesky.174
  1000.3 4.9 custom-call.16
  1011.6 35.9 %all-reduce.38 = bf16[64,1024]{1,0:T(8,128)(2,1)S(1)} all-reduce(f32[64,1024]{1,0:T(8,128)S(1)} %fusion.112), channel_id=1, replica_groups=mesh['gene'=8,'cell'=4] {'gene'}, use_global_device_ids=true, to_apply=%region_40.0 | all-reduce | flops 65536 | bytes 393216 | tf_op jit(solution)/shard_map/psum | solution.py:37
  1052.0 30.7 %all-reduce.29.cloned.1.call-done = bf16[64,2560]{1,0:T(8,128)(2,1)} async-done(((bf16[64,2560]{1,0:T(8,128)(2,1)}), bf16[64,2560]{1,0:T(8,128)(2,1)}) %all-reduce.29.cloned.1.call-update) | async-done | bytes 327696 | tf_op jit(solution)/shard_map/psum | solution.py:42
  1084.5 37.1 %psum.223 = f32[64,64]{0,1:T(8,128)S(1)} all-reduce(f32[64,64]{0,1:T(8,128)S(1)} %fusion.127), channel_id=1, replica_groups=mesh['gene'=8,'cell'=4] {'gene'}, use_global_device_ids=true, to_apply=%region_43.47 | all-reduce | flops 4096 | bytes 32768 | tf_op jit(solution)/shard_map/psum | solution.py:45
  1121.7 5.8 cholesky.185
  1128.9 4.9 custom-call.17
  (151 shorter events, 101.3 us)
Async XLA Ops:
  6.5 222.5 %all-reduce.31.cloned.1.call-start = ((), (), s32[]{:S(2)}) async-start(), calls=%async_computation.7 | async-start | bytes 172032 | tf_op jit(solution)/shard_map/psum | solution.py:32
  174.8 11.6 %slice-start = ((s8[5242880]{0:T(1024)(128)(4,1)}), s8[1048576]{0:T(1024)(128)(4,1)S(1)}, s32[]{:S(2)}) async-start(s8[5242880]{0:T(1024)(128)(4,1)} %bitcast.200), calls=%async_computation.8 | async-start | bytes 2097152
  179.0 7.3 slice-start.1
  179.0 12.7 %slice-start.2 = ((s8[5242880]{0:T(1024)(128)(4,1)}), s8[4194304]{0:T(1024)(128)(4,1)S(1)}, s32[]{:S(2)}) async-start(s8[5242880]{0:T(1024)(128)(4,1)} %bitcast.202), calls=%async_computation.10 | async-start | bytes 8388608
  179.0 12.7 %slice-start.4 = ((s8[5242880]{0:T(1024)(128)(4,1)}), s8[4194304]{0:T(1024)(128)(4,1)S(1)}, s32[]{:S(2)}) async-start(s8[5242880]{0:T(1024)(128)(4,1)} %bitcast.204), calls=%async_computation.12 | async-start | bytes 8388608
  186.3 5.4 slice-start.3
  186.3 5.4 slice-start.5
  191.8 38.0 %copy-start = (f32[64,2560]{1,0:T(8,128)S(1)}, f32[64,2560]{1,0:T(8,128)}, u32[]{:S(2)}) copy-start(f32[64,2560]{1,0:T(8,128)} %param.10) | copy-start | bytes 1966084
  195.5 114.6 %all-reduce.17.cloned.1.call-start = ((), (), s32[]{:S(2)}) async-start(), calls=%async_computation | async-start | bytes 655360 | tf_op jit(solution)/shard_map/psum | solution.py:42
  234.5 45.3 %copy-start.6 = (f32[2560]{0:T(1024)S(1)}, f32[2560]{0:T(1024)}, u32[]{:S(2)}) copy-start(f32[2560]{0:T(1024)} %get-tuple-element.8) | copy-start | bytes 30724
  279.8 159.0 %all-reduce.19.cloned.1.call-start = ((), (), s32[]{:S(2)}) async-start(), calls=%async_computation.1 | async-start | bytes 655360 | tf_op jit(solution)/shard_map/psum | solution.py:42
  367.6 40.6 %copy-start.5 = (f32[2560]{0:T(1024)S(1)}, f32[2560]{0:T(1024)}, u32[]{:S(2)}) copy-start(f32[2560]{0:T(1024)} %get-tuple-element.10) | copy-start | bytes 30724
  408.2 159.5 %all-reduce.21.cloned.1.call-start = ((), (), s32[]{:S(2)}) async-start(), calls=%async_computation.2 | async-start | bytes 655360 | tf_op jit(solution)/shard_map/psum | solution.py:42
  496.5 40.7 %copy-start.4 = (f32[2560]{0:T(1024)S(1)}, f32[2560]{0:T(1024)}, u32[]{:S(2)}) copy-start(f32[2560]{0:T(1024)} %get-tuple-element.11) | copy-start | bytes 30724
  537.1 159.3 %all-reduce.23.cloned.1.call-start = ((), (), s32[]{:S(2)}) async-start(), calls=%async_computation.3 | async-start | bytes 655360 | tf_op jit(solution)/shard_map/psum | solution.py:42
  625.1 40.9 %copy-start.3 = (f32[2560]{0:T(1024)S(1)}, f32[2560]{0:T(1024)}, u32[]{:S(2)}) copy-start(f32[2560]{0:T(1024)} %get-tuple-element.12) | copy-start | bytes 30724
  665.7 159.4 %all-reduce.25.cloned.1.call-start = ((), (), s32[]{:S(2)}) async-start(), calls=%async_computation.4 | async-start | bytes 655360 | tf_op jit(solution)/shard_map/psum | solution.py:42
  753.8 40.6 %copy-start.2 = (f32[2560]{0:T(1024)S(1)}, f32[2560]{0:T(1024)}, u32[]{:S(2)}) copy-start(f32[2560]{0:T(1024)} %get-tuple-element.13) | copy-start | bytes 30724
  794.4 159.7 %all-reduce.27.cloned.1.call-start = ((), (), s32[]{:S(2)}) async-start(), calls=%async_computation.5 | async-start | bytes 655360 | tf_op jit(solution)/shard_map/psum | solution.py:42
  882.6 40.9 %copy-start.1 = (f32[2560]{0:T(1024)S(1)}, f32[2560]{0:T(1024)}, u32[]{:S(2)}) copy-start(f32[2560]{0:T(1024)} %get-tuple-element.14) | copy-start | bytes 30724
  923.4 159.3 %all-reduce.29.cloned.1.call-start = ((), (), s32[]{:S(2)}) async-start(), calls=%async_computation.6 | async-start | bytes 655360 | tf_op jit(solution)/shard_map/psum | solution.py:42
Sparse Core Ops, SparseCore 0:
  195.6 33.3 all-reduce.30
  279.9 30.2 all-reduce.16
  408.3 30.4 all-reduce.18
  537.2 30.4 all-reduce.20
  665.8 30.5 all-reduce.22
  794.6 30.5 all-reduce.24
  923.5 30.5 all-reduce.26
  1052.1 30.5 all-reduce.28
where the time goes:
time: 1150 us; the launch traced here: 1140 us
  blocking collectives  517 us (45%)
  waiting for transfers between devices  247 us (21%)
  local copies, waits for them, and re-layouts  168 us (15%)
  other arithmetic  108 us (9%)
  matrix products  88.8 us (8%)
  between operations  14.6 us (1%)
    psum x7, blocking collectives, shards(): gram_matrix = lax.psum(gram_part, 'gene')  260 us
    psum x7, blocking collectives, shards(): scores = lax.psum(partial_value, 'gene')  257 us
    psum x7, waiting for transfers between devices, shards(): lax.psum(local_update.astype(jnp.bfloat16), 'cell').astype(jnp.float32)  214 us
    gather x7, local copies, waits for them, and re-layouts, shards(): gathered = jnp.take(pool_counts, chosen, axis=1)  141 us
    another operation x21, other arithmetic, shards(): factor = jnp.linalg.cholesky(gram_matrix)  45.6 us
    another operation x14, other arithmetic, shards(): lax.linalg.triangular_solve(factor, stepped, left_side=True, lower=True)  38.8 us
    psum x1, waiting for transfers between devices, shards(): batch_means = lax.psum(local_sums, 'cell') / batch_total  33.5 us
    dot_general x7, matrix products, transposed_product(): lax.dot_general(left, right, (((1,), (1,)), ((), ())), preferred_element_...  30.8 us
  transfers between devices with their start and end apart: 8, of which 8 were waited for; matrix products, arithmetic and copies ran while one was open for 0% of the time, Pallas kernels for 0%

commit v1 on v0

v1 whole, which is shorter than its diff:
```python
import functools
import math

import jax
import jax.numpy as jnp
from jax import lax
from jax.experimental import pallas as pl
from jax.experimental.pallas import tpu as pltpu
from jax.sharding import PartitionSpec as P

STEPS = 7
MESH = pl.DeviceIdType.MESH

step_rate = 1.0


def transposed_product(left, right):
    return lax.dot_general(
        left, right, (((1,), (1,)), ((), ())), preferred_element_type=jnp.float32
    )


def sum_kernel(axis, n, arrays, *refs):
    inputs, outputs = refs[:arrays], refs[arrays:2 * arrays]
    scratch = refs[2 * arrays:]
    landed, reduced, whole = (scratch[i * arrays:(i + 1) * arrays] for i in range(3))
    sends, arrivals, sends_back, arrivals_back = scratch[3 * arrays:]
    me = lax.axis_index(axis)
    barrier = pltpu.get_barrier_semaphore()
    peers = [lax.rem(me + k, n) for k in range(n)]
    for k in range(1, n):
        pl.semaphore_signal(barrier, inc=1, device_id={axis: peers[k]}, device_id_type=MESH)
    pl.semaphore_wait(barrier, n - 1)
    copies = []
    for a in range(arrays):
        for k in range(1, n):
            copy = pltpu.make_async_remote_copy(
                src_ref=inputs[a].at[peers[k]],
                dst_ref=landed[a].at[k - 1],
                send_sem=sends.at[a, k - 1],
                recv_sem=arrivals.at[a, k - 1],
                device_id={axis: peers[k]},
                device_id_type=MESH,
            )
            copy.start()
            copies.append(copy)
    for copy in copies:
        copy.wait_recv()
    backs = []
    for a in range(arrays):
        total = inputs[a][me].astype(jnp.float32)
        for k in range(1, n):
            total = total + landed[a][k - 1].astype(jnp.float32)
        reduced[a][...] = total.astype(reduced[a].dtype)
        for k in range(1, n):
            copy = pltpu.make_async_remote_copy(
                src_ref=reduced[a],
                dst_ref=whole[a].at[me],
                send_sem=sends_back.at[a, k - 1],
                recv_sem=arrivals_back.at[a, k - 1],
                device_id={axis: peers[k]},
                device_id_type=MESH,
            )
            copy.start()
            backs.append(copy)
        outputs[a][me] = reduced[a][...]
    for copy in copies:
        copy.wait_send()
    for copy in backs:
        copy.wait()
    for a in range(arrays):
        for k in range(1, n):
            outputs[a][peers[k]] = whole[a][peers[k]]


def sum_over(axis, n, collective_id, *arrays):
    cut = [a.reshape(n, a.shape[0] // n, a.shape[1]) for a in arrays]
    count = len(cut)
    scratch = [pltpu.VMEM((n - 1,) + a.shape[1:], a.dtype) for a in cut]
    scratch += [pltpu.VMEM(a.shape[1:], a.dtype) for a in cut]
    scratch += [pltpu.VMEM(a.shape, a.dtype) for a in cut]
    scratch += [pltpu.SemaphoreType.DMA((count, n - 1))] * 4
    outs = pl.pallas_call(
        functools.partial(sum_kernel, axis, n, count),
        out_shape=[jax.ShapeDtypeStruct(a.shape, a.dtype) for a in cut],
        in_specs=[pl.BlockSpec(memory_space=pltpu.VMEM)] * count,
        out_specs=[pl.BlockSpec(memory_space=pltpu.VMEM)] * count,
        scratch_shapes=scratch,
        compiler_params=pltpu.CompilerParams(
            collective_id=collective_id, has_side_effects=True
        ),
        name=f"sum_{axis}_{collective_id}",
    )(*cut)
    return [o.reshape(a.shape) for o, a in zip(outs, arrays)]


def inverse_factor(gram):
    size = gram.shape[0]
    rows = lax.broadcasted_iota(jnp.int32, (size, size), 0)
    columns = lax.broadcasted_iota(jnp.int32, (size, size), 1)
    left = gram
    right = jnp.where(rows == columns, 1.0, 0.0).astype(jnp.float32)
    for k in range(size):
        scale = 1.0 / jnp.sqrt(left[k:k + 1, k:k + 1])
        column = jnp.where(rows[:, :1] > k, left[:, k:k + 1] * scale, 0.0)
        left_row = left[k:k + 1, :] * scale
        right_row = right[k:k + 1, :] * scale
        left = left - column * left_row
        right = jnp.where(rows == k, right_row, right - column * right_row)
    return right


def exact_product(left, right):
    return jnp.dot(
        left, right, precision=lax.Precision.HIGHEST, preferred_element_type=jnp.float32
    )


def normalise_kernel(gram_ref, stepped_ref, *refs):
    inverse = inverse_factor(gram_ref[...])
    if len(refs) == 1:
        refs[0][...] = exact_product(inverse, stepped_ref[...])
        return
    raw_ref, loadings_ref, scores_ref = refs
    scores_ref[...] = exact_product(inverse, raw_ref[...].astype(jnp.float32)).astype(
        scores_ref.dtype
    )
    loadings_ref[...] = exact_product(inverse, stepped_ref[...])


def normalise(gram, stepped, raw=None):
    shapes = [jax.ShapeDtypeStruct(stepped.shape, jnp.float32)]
    operands = [gram, stepped]
    if raw is not None:
        shapes.append(jax.ShapeDtypeStruct(raw.shape, jnp.bfloat16))
        operands.append(raw)
    return pl.pallas_call(
        normalise_kernel,
        out_shape=shapes,
        in_specs=[pl.BlockSpec(memory_space=pltpu.VMEM)] * len(operands),
        out_specs=[pl.BlockSpec(memory_space=pltpu.VMEM)] * len(shapes),
        name="normalise",
    )(*operands)


def shards(genes, cells, pool_counts, cell_picks, loadings_init):
    stepped = loadings_init
    local_pool = pool_counts.shape[1]
    group = lax.axis_index("cell")
    batch_total = cell_picks.shape[1] * cells
    gene_total = stepped.shape[1] * genes
    tiles = [
        jnp.take(pool_counts, cell_picks[s] - group * local_pool, axis=1, mode="clip")
        for s in range(STEPS)
    ]
    sums = [jnp.sum(tile, axis=1, dtype=jnp.float32) for tile in tiles]
    padded = -(-STEPS // cells) * cells
    sums += [jnp.zeros_like(sums[0])] * (padded - STEPS)
    (totals,) = sum_over("cell", cells, 1, jnp.stack(sums))
    means = totals / batch_total
    for s in range(STEPS):
        mean = means[s]
        low = stepped.astype(jnp.bfloat16)
        product = jnp.dot(low, tiles[s], preferred_element_type=jnp.float32)
        shift = jnp.dot(low.astype(jnp.float32), mean, precision=lax.Precision.HIGHEST)
        part = (product - shift[:, None]).astype(jnp.bfloat16)
        if s == 0:
            (scores_low,) = sum_over("gene", genes, 2, part)
            loadings = stepped
        else:
            gram_part = jnp.dot(stepped, stepped.T, precision=lax.Precision.HIGHEST)
            raw, gram = sum_over("gene", genes, 3, part, gram_part)
            loadings, scores_low = normalise(gram, stepped, raw)
        raw_update = transposed_product(scores_low, tiles[s])
        row_totals = jnp.sum(scores_low, axis=1, dtype=jnp.float32)
        local = (raw_update - row_totals[:, None] * mean[None, :]) / batch_total
        (update,) = sum_over("cell", cells, 4, local.astype(jnp.bfloat16))
        stepped = loadings + step_rate * update.astype(jnp.float32)
    gram_part = jnp.dot(stepped, stepped.T, precision=lax.Precision.HIGHEST)
    (gram,) = sum_over("gene", genes, 5, gram_part)
    (loadings,) = normalise(gram, stepped)
    return loadings * math.sqrt(gene_total)


def solution(mesh):
    placed = (P("gene", "cell"), P(None, "cell"), P(None, "gene"))
    return jax.shard_map(
        functools.partial(shards, mesh.shape["gene"], mesh.shape["cell"]),
        mesh=mesh, in_specs=placed, out_specs=P(None, "gene"), check_vma=False,
    )
```

time: 1150 us -> 572 us (0.50)
  blocking collectives: 517 us -> 0 us
  Pallas kernels: 0 us -> 282 us
  waiting for transfers between devices: 247 us -> 0 us
  other arithmetic: 108 us -> 33.6 us
  between operations: 14.6 us -> 1.02 us
  matrix products: 88.8 us -> 75.7 us
    psum x14 -> x0, blocking collectives: 517 us -> none  [the longest x7 260 us: shards(): gram_matrix = lax.psum(gram_part, 'gene')]
    pallas_call x0 -> x23, Pallas kernels: none -> 282 us  [the longest x16 220 us: sum_over(): pl.pallas_call(functools.partial(sum_kernel, axis, n, count), out_shape=[...]
    psum x8 -> x0, waiting for transfers between devices: 247 us -> none  [the longest x7 214 us: shards(): lax.psum(local_update.astype(jnp.bfloat16), 'cell').astype(jnp.float32)]
    another operation x35 -> x0, other arithmetic: 84.5 us -> none  [the longest x21 45.6 us: shards(): factor = jnp.linalg.cholesky(gram_matrix)]
    another operation x7 -> x0, matrix products: 12.9 us -> none  [shards(): lax.linalg.triangular_solve(factor, stepped, left_side=True, lower=True)]
    unnamed x27 -> x43, local copies, waits for them, and re-layouts: 25.9 us -> 26 us
  transfers between devices with their start and end apart: 8 -> 0, of which waited for: 8 -> 0; matrix products, arithmetic and copies ran while one was open for 0% -> 0% of each run, Pallas kernels for 0% -> 0%
where the time goes in v1:
time: 572 us; the launch traced here: 561 us
  Pallas kernels  282 us (49%)
  local copies, waits for them, and re-layouts  169 us (30%)
  matrix products  75.7 us (13%)
  other arithmetic  33.6 us (6%)
    pallas_call x16, Pallas kernels, sum_over(): pl.pallas_call(functools.partial(sum_kernel, axis, n, count), out_shape=[...  220 us
    gather x7, local copies, waits for them, and re-layouts, shards(): jnp.take(pool_counts, cell_picks[s] - group * local_pool, axis=1, mode='c...  141 us
    pallas_call x7, Pallas kernels, normalise(): pl.pallas_call(normalise_kernel, out_shape=shapes, in_specs=[pl.BlockSpec...  62.9 us
    dot_general x7, matrix products, shards(): product = jnp.dot(low, tiles[s], preferred_element_type=jnp.float32)  33.9 us
    dot_general x7, matrix products, transposed_product(): lax.dot_general(left, right, (((1,), (1,)), ((), ())), preferred_element_...  30.3 us
    unnamed x43, local copies, waits for them, and re-layouts  26 us
    reduce_sum x7, other arithmetic, shards(): sums = [jnp.sum(tile, axis=1, dtype=jnp.float32) for tile in tiles]  15.9 us

profile of v1, /device:TPU:0, one launch (start us, length us, event | category | flops | bytes accessed | tf_op | source)
XLA Modules:
  0.0 561.5 jit_solution(8170381645345899886)
XLA Ops:
  0.0 25.9 %copy.4 = bf16[2560,4096]{0,1:T(8,128)(2,1)} copy(bf16[2560,4096]{1,0:T(8,128)(2,1)} %param.3) | data formatting | bytes 41943040 | tf_op args[0]
  25.9 20.2 %gather_fusion.6 = bf16[1024,2560]{1,0:T(8,128)(2,1)} fusion(bf16[2560,4096]{0,1:T(8,128)(2,1)} %copy.4, s32[1024]{0:T(1024)S(1)} %broadcast_clamp_fusion), kind=kCustom, calls=%fused_computation.6 | custom fusion | bytes 10489856 | tf_op jit(solution)/shard_map/jit(_take)/gather | solution.py:153
  46.1 20.1 %gather_fusion.5 = bf16[1024,2560]{1,0:T(8,128)(2,1)} fusion(bf16[2560,4096]{0,1:T(8,128)(2,1)} %copy.4, s32[1024]{0:T(1024)S(1)} %broadcast_clamp_fusion.1), kind=kCustom, calls=%fused_computation.5 | custom fusion | bytes 10489856 | tf_op jit(solution)/shard_map/jit(_take)/gather | solution.py:153
  66.2 20.3 %gather_fusion.4 = bf16[1024,2560]{1,0:T(8,128)(2,1)} fusion(bf16[2560,4096]{0,1:T(8,128)(2,1)} %copy.4, s32[1024]{0:T(1024)S(1)} %broadcast_clamp_fusion.2), kind=kCustom, calls=%fused_computation.4 | custom fusion | bytes 10489856 | tf_op jit(solution)/shard_map/jit(_take)/gather | solution.py:153
  86.5 20.1 %gather_fusion.3 = bf16[1024,2560]{1,0:T(8,128)(2,1)} fusion(bf16[2560,4096]{0,1:T(8,128)(2,1)} %copy.4, s32[1024]{0:T(1024)S(1)} %broadcast_clamp_fusion.3), kind=kCustom, calls=%fused_computation.3 | custom fusion | bytes 10489856 | tf_op jit(solution)/shard_map/jit(_take)/gather | solution.py:153
  106.6 20.3 %gather_fusion.2 = bf16[1024,2560]{1,0:T(8,128)(2,1)} fusion(bf16[2560,4096]{0,1:T(8,128)(2,1)} %copy.4, s32[1024]{0:T(1024)S(1)} %broadcast_clamp_fusion.4), kind=kCustom, calls=%fused_computation.2 | custom fusion | bytes 10489856 | tf_op jit(solution)/shard_map/jit(_take)/gather | solution.py:153
  126.9 20.1 %gather_fusion.1 = bf16[1024,2560]{1,0:T(8,128)(2,1)} fusion(bf16[2560,4096]{0,1:T(8,128)(2,1)} %copy.4, s32[1024]{0:T(1024)S(1)} %broadcast_clamp_fusion.5), kind=kCustom, calls=%fused_computation.1 | custom fusion | bytes 10489856 | tf_op jit(solution)/shard_map/jit(_take)/gather | solution.py:153
  147.0 20.5 %gather_fusion = bf16[1024,2560]{1,0:T(8,128)(2,1)} fusion(bf16[2560,4096]{0,1:T(8,128)(2,1)} %copy.4, s32[1024]{0:T(1024)S(1)} %broadcast_clamp_fusion.6), kind=kCustom, calls=%fused_computation | custom fusion | bytes 10489856 | tf_op jit(solution)/shard_map/jit(_take)/gather | solution.py:153
  167.5 3.4 convert_reduce_fusion.6
  170.9 3.4 convert_reduce_fusion.5
  177.8 3.4 convert_reduce_fusion.3
  184.5 10.2 %sum_cell_1.1 = f32[4,2,2560]{2,1,0:T(2,128)} custom-call(f32[4,2,2560]{2,1,0:T(2,128)} %reshape.232.refs_0_), custom_call_target="tpu_custom_call" | custom-call | tf_op jit(solution)/shard_map/sum_cell_1/pallas_call | solution.py:83
  196.2 4.9 fusion.27.refs_0_
  201.0 15.6 %sum_gene_2.1 = bf16[8,8,1024]{2,1,0:T(8,128)(2,1)} custom-call(bf16[8,8,1024]{2,1,0:T(8,128)(2,1)} %fusion.27.refs_0_), custom_call_target="tpu_custom_call" | custom-call | tf_op jit(solution)/shard_map/sum_gene_2/pallas_call | solution.py:83
  217.7 4.3 fusion.13
  222.1 11.4 %sum_cell_4.7 = bf16[4,16,2560]{2,1,0:T(8,128)(2,1)} custom-call(bf16[4,16,2560]{2,1,0:T(8,128)(2,1)} %bitcast.156), custom_call_target="tpu_custom_call" | custom-call | tf_op jit(solution)/shard_map/sum_cell_4/pallas_call | solution.py:83
  234.9 4.8 fusion.26.refs_0_
  241.0 16.5 %sum_gene_3.6 = (bf16[8,8,1024]{2,1,0:T(8,128)(2,1)}, f32[8,8,64]{2,1,0:T(8,128)}) custom-call(bf16[8,8,1024]{2,1,0:T(8,128)(2,1)} %fusion.26.refs_0_, f32[8,8,64]{2,1,0:T(8,128)} %convolution_bitcast_fusion.6.refs_1_), custom_call_target="tpu_custom_call" | custom-call | tf_op jit(solution)/shard_map/sum_gene_3/pallas_call | solution.py:83
  257.6 9.2 %normalise.7 = (f32[64,2560]{1,0:T(8,128)}, bf16[64,1024]{1,0:T(8,128)(2,1)}) custom-call(f32[64,64]{1,0:T(8,128)} %bitcast.170, f32[64,2560]{1,0:T(8,128)} %copy-done.5, bf16[64,1024]{1,0:T(8,128)(2,1)} %bitcast.163), custom_call_target="tpu_custom_call" | custom-call | tf_op jit(solution)/shard_map/normalise/pallas_call | solution.py:137
  267.8 4.3 fusion.12
  272.2 11.9 %sum_cell_4.8 = bf16[4,16,2560]{2,1,0:T(8,128)(2,1)} custom-call(bf16[4,16,2560]{2,1,0:T(8,128)(2,1)} %bitcast.157), custom_call_target="tpu_custom_call" | custom-call | tf_op jit(solution)/shard_map/sum_cell_4/pallas_call | solution.py:83
  285.5 4.8 fusion.25.refs_0_
  291.6 16.7 %sum_gene_3.7 = (bf16[8,8,1024]{2,1,0:T(8,128)(2,1)}, f32[8,8,64]{2,1,0:T(8,128)}) custom-call(bf16[8,8,1024]{2,1,0:T(8,128)(2,1)} %fusion.25.refs_0_, f32[8,8,64]{2,1,0:T(8,128)} %convolution_bitcast_fusion.5.refs_1_), custom_call_target="tpu_custom_call" | custom-call | tf_op jit(solution)/shard_map/sum_gene_3/pallas_call | solution.py:83
  308.3 9.0 %normalise.8 = (f32[64,2560]{1,0:T(8,128)}, bf16[64,1024]{1,0:T(8,128)(2,1)}) custom-call(f32[64,64]{1,0:T(8,128)} %bitcast.171, f32[64,2560]{1,0:T(8,128)} %copy-done.1, bf16[64,1024]{1,0:T(8,128)(2,1)} %bitcast.164), custom_call_target="tpu_custom_call" | custom-call | tf_op jit(solution)/shard_map/normalise/pallas_call | solution.py:137
  318.4 4.3 fusion.11
  322.7 11.5 %sum_cell_4.9 = bf16[4,16,2560]{2,1,0:T(8,128)(2,1)} custom-call(bf16[4,16,2560]{2,1,0:T(8,128)(2,1)} %bitcast.158), custom_call_target="tpu_custom_call" | custom-call | tf_op jit(solution)/shard_map/sum_cell_4/pallas_call | solution.py:83
  335.6 4.8 fusion.24.refs_0_
  341.7 16.5 %sum_gene_3.8 = (bf16[8,8,1024]{2,1,0:T(8,128)(2,1)}, f32[8,8,64]{2,1,0:T(8,128)}) custom-call(bf16[8,8,1024]{2,1,0:T(8,128)(2,1)} %fusion.24.refs_0_, f32[8,8,64]{2,1,0:T(8,128)} %convolution_bitcast_fusion.4.refs_1_), custom_call_target="tpu_custom_call" | custom-call | tf_op jit(solution)/shard_map/sum_gene_3/pallas_call | solution.py:83
  358.3 9.0 %normalise.9 = (f32[64,2560]{1,0:T(8,128)}, bf16[64,1024]{1,0:T(8,128)(2,1)}) custom-call(f32[64,64]{1,0:T(8,128)} %bitcast.172, f32[64,2560]{1,0:T(8,128)} %copy-done.2, bf16[64,1024]{1,0:T(8,128)(2,1)} %bitcast.165), custom_call_target="tpu_custom_call" | custom-call | tf_op jit(solution)/shard_map/normalise/pallas_call | solution.py:137
  368.3 4.3 fusion.10
  372.7 12.2 %sum_cell_4.10 = bf16[4,16,2560]{2,1,0:T(8,128)(2,1)} custom-call(bf16[4,16,2560]{2,1,0:T(8,128)(2,1)} %bitcast.159), custom_call_target="tpu_custom_call" | custom-call | tf_op jit(solution)/shard_map/sum_cell_4/pallas_call | solution.py:83
  386.2 4.8 fusion.23.refs_0_
  392.3 16.7 %sum_gene_3.9 = (bf16[8,8,1024]{2,1,0:T(8,128)(2,1)}, f32[8,8,64]{2,1,0:T(8,128)}) custom-call(bf16[8,8,1024]{2,1,0:T(8,128)(2,1)} %fusion.23.refs_0_, f32[8,8,64]{2,1,0:T(8,128)} %convolution_bitcast_fusion.3.refs_1_), custom_call_target="tpu_custom_call" | custom-call | tf_op jit(solution)/shard_map/sum_gene_3/pallas_call | solution.py:83
  409.0 9.0 %normalise.10 = (f32[64,2560]{1,0:T(8,128)}, bf16[64,1024]{1,0:T(8,128)(2,1)}) custom-call(f32[64,64]{1,0:T(8,128)} %bitcast.173, f32[64,2560]{1,0:T(8,128)} %copy-done.3, bf16[64,1024]{1,0:T(8,128)(2,1)} %bitcast.166), custom_call_target="tpu_custom_call" | custom-call | tf_op jit(solution)/shard_map/normalise/pallas_call | solution.py:137
  419.1 4.3 fusion.9
  423.5 11.5 %sum_cell_4.11 = bf16[4,16,2560]{2,1,0:T(8,128)(2,1)} custom-call(bf16[4,16,2560]{2,1,0:T(8,128)(2,1)} %bitcast.160), custom_call_target="tpu_custom_call" | custom-call | tf_op jit(solution)/shard_map/sum_cell_4/pallas_call | solution.py:83
  436.4 4.8 fusion.22.refs_0_
  442.5 16.5 %sum_gene_3.10 = (bf16[8,8,1024]{2,1,0:T(8,128)(2,1)}, f32[8,8,64]{2,1,0:T(8,128)}) custom-call(bf16[8,8,1024]{2,1,0:T(8,128)(2,1)} %fusion.22.refs_0_, f32[8,8,64]{2,1,0:T(8,128)} %convolution_bitcast_fusion.2.refs_1_), custom_call_target="tpu_custom_call" | custom-call | tf_op jit(solution)/shard_map/sum_gene_3/pallas_call | solution.py:83
  459.0 9.0 %normalise.11 = (f32[64,2560]{1,0:T(8,128)}, bf16[64,1024]{1,0:T(8,128)(2,1)}) custom-call(f32[64,64]{1,0:T(8,128)} %bitcast.174, f32[64,2560]{1,0:T(8,128)} %copy-done.4, bf16[64,1024]{1,0:T(8,128)(2,1)} %bitcast.167), custom_call_target="tpu_custom_call" | custom-call | tf_op jit(solution)/shard_map/normalise/pallas_call | solution.py:137
  469.1 4.3 fusion.8
  473.4 11.9 %sum_cell_4.12 = bf16[4,16,2560]{2,1,0:T(8,128)(2,1)} custom-call(bf16[4,16,2560]{2,1,0:T(8,128)(2,1)} %bitcast.161), custom_call_target="tpu_custom_call" | custom-call | tf_op jit(solution)/shard_map/sum_cell_4/pallas_call | solution.py:83
  486.8 4.8 fusion.21.refs_0_
  493.1 16.7 %sum_gene_3.11 = (bf16[8,8,1024]{2,1,0:T(8,128)(2,1)}, f32[8,8,64]{2,1,0:T(8,128)}) custom-call(bf16[8,8,1024]{2,1,0:T(8,128)(2,1)} %fusion.21.refs_0_, f32[8,8,64]{2,1,0:T(8,128)} %convolution_bitcast_fusion.1.refs_1_), custom_call_target="tpu_custom_call" | custom-call | tf_op jit(solution)/shard_map/sum_gene_3/pallas_call | solution.py:83
  509.8 9.0 %normalise.12 = (f32[64,2560]{1,0:T(8,128)}, bf16[64,1024]{1,0:T(8,128)(2,1)}) custom-call(f32[64,64]{1,0:T(8,128)} %bitcast.175, f32[64,2560]{1,0:T(8,128)} %copy-done, bf16[64,1024]{1,0:T(8,128)(2,1)} %bitcast.168), custom_call_target="tpu_custom_call" | custom-call | tf_op jit(solution)/shard_map/normalise/pallas_call | solution.py:137
  519.9 4.3 fusion.7
  524.3 11.5 %sum_cell_4.13 = bf16[4,16,2560]{2,1,0:T(8,128)(2,1)} custom-call(bf16[4,16,2560]{2,1,0:T(8,128)(2,1)} %bitcast.162), custom_call_target="tpu_custom_call" | custom-call | tf_op jit(solution)/shard_map/sum_cell_4/pallas_call | solution.py:83
  538.1 12.1 %sum_gene_5.1 = f32[8,8,64]{2,1,0:T(8,128)} custom-call(f32[8,8,64]{2,1,0:T(8,128)} %convolution_bitcast_fusion.refs_0_), custom_call_target="tpu_custom_call" | custom-call | tf_op jit(solution)/shard_map/sum_gene_5/pallas_call | solution.py:83
  550.2 8.8 %normalise.13 = f32[64,2560]{1,0:T(8,128)} custom-call(f32[64,64]{1,0:T(8,128)} %bitcast.169, f32[64,2560]{1,0:T(8,128)} %copy-done.6), custom_call_target="tpu_custom_call" | custom-call | tf_op jit(solution)/shard_map/normalise/pallas_call | solution.py:137
  (100 shorter events, 36.3 us)
Async XLA Ops:
  0.0 25.9 %copy-start.14 = (s32[7,1024]{1,0:T(8,128)S(1)}, s32[7,1024]{1,0:T(8,128)}, u32[]{:S(2)}) copy-start(s32[7,1024]{1,0:T(8,128)} %param.4) | copy-start | bytes 86020
  167.4 14.5 %slice-start.2 = ((s8[5242880]{0:T(1024)(128)(4,1)}), s8[4194304]{0:T(1024)(128)(4,1)S(1)}, s32[]{:S(2)}) async-start(s8[5242880]{0:T(1024)(128)(4,1)} %bitcast.152), calls=%async_computation.2 | async-start | bytes 8388608
  170.9 10.3 %slice-start.4 = ((s8[5242880]{0:T(1024)(128)(4,1)}), s8[4194304]{0:T(1024)(128)(4,1)S(1)}, s32[]{:S(2)}) async-start(s8[5242880]{0:T(1024)(128)(4,1)} %bitcast.154), calls=%async_computation.4 | async-start | bytes 8388608
  174.3 6.9 %slice-start.5 = ((s8[5242880]{0:T(1024)(128)(4,1)}), s8[1048576]{0:T(1024)(128)(4,1)S(1)}, s32[]{:S(2)}) async-start(s8[5242880]{0:T(1024)(128)(4,1)} %bitcast.154), calls=%async_computation.5 | async-start | bytes 2097152
  174.3 7.7 %slice-start.3 = ((s8[5242880]{0:T(1024)(128)(4,1)}), s8[1048576]{0:T(1024)(128)(4,1)S(1)}, s32[]{:S(2)}) async-start(s8[5242880]{0:T(1024)(128)(4,1)} %bitcast.152), calls=%async_computation.3 | async-start | bytes 2097152
  177.7 5.1 slice-start
  181.2 1.6 slice-start.1
  182.0 13.8 %copy-start.7 = (f32[64,2560]{1,0:T(8,128)S(1)}, f32[64,2560]{1,0:T(8,128)}, u32[]{:S(2)}) copy-start(f32[64,2560]{1,0:T(8,128)} %param.5) | copy-start | bytes 1966084
  234.6 23.0 %copy-start.5 = (f32[64,2560]{1,0:T(8,128)}, f32[64,2560]{1,0:T(8,128)S(1)}, u32[]{:S(2)}) copy-start(f32[64,2560]{1,0:T(8,128)S(1)} %convert_add_fusion.6.stepped_ref) | copy-start | bytes 1966084
  266.7 17.4 %copy-start.9 = (f32[64,2560]{1,0:T(8,128)S(1)}, f32[64,2560]{1,0:T(8,128)}, u32[]{:S(2)}) copy-start(f32[64,2560]{1,0:T(8,128)} %get-tuple-element.31) | copy-start | bytes 1966084
  285.1 23.2 %copy-start.1 = (f32[64,2560]{1,0:T(8,128)}, f32[64,2560]{1,0:T(8,128)S(1)}, u32[]{:S(2)}) copy-start(f32[64,2560]{1,0:T(8,128)S(1)} %convert_add_fusion.5.stepped_ref) | copy-start | bytes 1966084
  317.3 16.9 %copy-start.10 = (f32[64,2560]{1,0:T(8,128)S(1)}, f32[64,2560]{1,0:T(8,128)}, u32[]{:S(2)}) copy-start(f32[64,2560]{1,0:T(8,128)} %get-tuple-element.35) | copy-start | bytes 1966084
  335.3 23.0 %copy-start.2 = (f32[64,2560]{1,0:T(8,128)}, f32[64,2560]{1,0:T(8,128)S(1)}, u32[]{:S(2)}) copy-start(f32[64,2560]{1,0:T(8,128)S(1)} %convert_add_fusion.4.stepped_ref) | copy-start | bytes 1966084
  367.3 17.6 %copy-start.11 = (f32[64,2560]{1,0:T(8,128)S(1)}, f32[64,2560]{1,0:T(8,128)}, u32[]{:S(2)}) copy-start(f32[64,2560]{1,0:T(8,128)} %get-tuple-element.39) | copy-start | bytes 1966084
  385.9 23.2 %copy-start.3 = (f32[64,2560]{1,0:T(8,128)}, f32[64,2560]{1,0:T(8,128)S(1)}, u32[]{:S(2)}) copy-start(f32[64,2560]{1,0:T(8,128)S(1)} %convert_add_fusion.3.stepped_ref) | copy-start | bytes 1966084
  418.0 16.9 %copy-start.12 = (f32[64,2560]{1,0:T(8,128)S(1)}, f32[64,2560]{1,0:T(8,128)}, u32[]{:S(2)}) copy-start(f32[64,2560]{1,0:T(8,128)} %get-tuple-element.43) | copy-start | bytes 1966084
  436.0 23.0 %copy-start.4 = (f32[64,2560]{1,0:T(8,128)}, f32[64,2560]{1,0:T(8,128)S(1)}, u32[]{:S(2)}) copy-start(f32[64,2560]{1,0:T(8,128)S(1)} %convert_add_fusion.2.stepped_ref) | copy-start | bytes 1966084
  468.0 17.4 %copy-start.13 = (f32[64,2560]{1,0:T(8,128)S(1)}, f32[64,2560]{1,0:T(8,128)}, u32[]{:S(2)}) copy-start(f32[64,2560]{1,0:T(8,128)} %get-tuple-element.47) | copy-start | bytes 1966084
  486.4 23.4 %copy-start = (f32[64,2560]{1,0:T(8,128)}, f32[64,2560]{1,0:T(8,128)S(1)}, u32[]{:S(2)}) copy-start(f32[64,2560]{1,0:T(8,128)S(1)} %convert_add_fusion.1.stepped_ref) | copy-start | bytes 1966084
  518.8 16.9 %copy-start.8 = (f32[64,2560]{1,0:T(8,128)S(1)}, f32[64,2560]{1,0:T(8,128)}, u32[]{:S(2)}) copy-start(f32[64,2560]{1,0:T(8,128)} %get-tuple-element.51) | copy-start | bytes 1966084
  536.8 13.4 %copy-start.6 = (f32[64,2560]{1,0:T(8,128)}, f32[64,2560]{1,0:T(8,128)S(1)}, u32[]{:S(2)}) copy-start(f32[64,2560]{1,0:T(8,128)S(1)} %convert_add_fusion.stepped_ref) | copy-start | bytes 1966084
